TPU v7x, 32 devices: a whole 2x2x4 slice. The times are simulated.
32 devices in a mesh: mu: 8 (over y, x, core), nu: 4 (over z).
Axes of the slice: x: 2, y: 2, z: 4, core: 2. Of those that a mesh axis runs over, the one named last changes fastest.
Arguments:
- earlier_vectors: float32 [1024, 1024, 512], P('mu', 'nu'), may hold values from -0.72 to 0.72
- pivot_integral_columns: float32 [1024, 1024, 256], P('mu', 'nu'), may hold values from -6 to 6
- diagonal: float32 [1024, 1024], P('mu', 'nu'), may hold values from 2 to 60
- orbitals: float32 [1024, 40], replicated, may hold values from -0.1875 to 0.1875
- pivots: int32 [256], replicated, may hold values from 0 to 1048575, as said below
Outputs:
- transformed: float32 [256, 820], P(('mu', 'nu'))
- updated_diagonal: float32 [1024, 1024], P('mu', 'nu')
Inputs may be any that keep to these rules, and one draw needn't show every extreme that they name: The pivots are distinct. The pairs held by one device (a block of 128 first by 256 second AO indices) contain at most 32 pivots, and some block contains exactly 32.
All inputs are finite; a program needn't handle non-finite values.
Results may differ from a plain program's by a relative error of at most 0.0001.
Values sent between devices are 32-bit elements; how exact they have to be, the bound alone decides.
A program may use at most 256 MiB of HBM per device.

v0:
```python
import jax
import jax.numpy as jnp
import numpy as np
from jax import lax
from jax.sharding import PartitionSpec as P

precise = lax.Precision.HIGHEST


def local(earlier_vectors, pivot_integral_columns, diagonal, orbitals, pivots):
    orbital_rows_mu, cols_nu, preceding = earlier_vectors.shape
    pivot_count = pivots.shape[0]
    ao_count, active = orbitals.shape
    size_mu = lax.axis_size("mu")
    size_nu = lax.axis_size("nu")
    index_mu = lax.axis_index("mu")
    index_nu = lax.axis_index("nu")
    pivot_mu = pivots // ao_count
    pivot_nu = pivots % ao_count
    owner_mu = pivot_mu // orbital_rows_mu
    owner_nu = pivot_nu // cols_nu
    local_row = pivot_mu % orbital_rows_mu * cols_nu + pivot_nu % cols_nu
    is_owned = (owner_mu == index_mu) & (owner_nu == index_nu)
    flat_vectors = earlier_vectors.reshape(orbital_rows_mu * cols_nu, preceding)
    flat_diag = diagonal.reshape(orbital_rows_mu * cols_nu)
    picked = jnp.take(flat_vectors, local_row, axis=0)
    picked_diag = jnp.take(flat_diag, local_row)
    masked = jnp.where(is_owned[:, None], picked, 0.0)
    masked_diag = jnp.where(is_owned, picked_diag, 0.0)
    pivot_rows, pivot_diag = lax.psum((masked, masked_diag), ("mu", "nu"))
    residual_diag = pivot_diag - jnp.sum(pivot_rows * pivot_rows, axis=1)
    scaling = lax.rsqrt(jnp.maximum(residual_diag, 1.0))
    update = lax.dot_general(flat_vectors, pivot_rows, (((1,), (1,)), ((), ())), precision=precise)
    flat_columns = pivot_integral_columns.reshape(orbital_rows_mu * cols_nu, pivot_count)
    fresh_vectors = (flat_columns - update) * scaling[None, :]
    updated_diagonal = (flat_diag - jnp.sum(fresh_vectors * fresh_vectors, axis=1)).reshape(
        orbital_rows_mu, cols_nu
    )
    basis_left_index = lax.dynamic_slice_in_dim(
        orbitals, index_mu * orbital_rows_mu, orbital_rows_mu, 0
    )
    orbit_nu = lax.dynamic_slice_in_dim(orbitals, index_nu * cols_nu, cols_nu, 0)
    fresh_blocks = fresh_vectors.reshape(orbital_rows_mu, cols_nu, pivot_count)
    half_done = jnp.einsum("mp,mnj->jpn", basis_left_index, fresh_blocks, precision=precise)
    row_index, col_index = np.tril_indices(active)
    full_done = jnp.einsum("nq,jpn->jpq", orbit_nu, half_done, precision=precise)
    pair_values = full_done[:, row_index, col_index]
    pair_count = row_index.shape[0]
    per_device = pivot_count // (size_mu * size_nu)
    split_mu = pair_values.reshape(size_mu, size_nu * per_device, pair_count)
    summed = lax.psum_scatter(split_mu, "mu", scatter_dimension=0, tiled=True)
    split_nu = summed.reshape(size_nu, per_device, pair_count)
    transformed = lax.psum_scatter(split_nu, "nu", scatter_dimension=0, tiled=True).reshape(
        per_device, pair_count
    )
    return (transformed, updated_diagonal)


def solution(mesh):
    placed = (P("mu", "nu", None), P("mu", "nu", None), P("mu", "nu"), P(), P())
    return jax.shard_map(
        local,
        mesh=mesh,
        in_specs=placed,
        out_specs=(P(("mu", "nu"), None), P("mu", "nu")),
        check_vma=False,
    )
```

profile of v0, /device:TPU:0, one launch (start us, length us, event | category | flops | bytes accessed | tf_op | source)
XLA Modules:
  0.0 358.0 jit_solution(5363346834168782279)
XLA Ops:
  7.2 0.0 copy-start
  7.2 0.0 all-reduce.3.cloned.1.call-start
  7.2 0.7 compare_select_fusion
  8.0 1.0 copy.21
  9.0 1.7 gather_fusion.1
  10.7 2.8 gather_fusion
  13.5 0.7 select_select_fusion.1
  14.2 0.9 select_select_fusion
  15.1 0.0 all-reduce.3.cloned.1.call-update
  15.1 0.0 reduce-scatter.5.cloned.1.call-start
  15.2 31.1 %copy.20 = f32[32768,256]{0,1:T(8,128)} copy(f32[32768,256]{1,0:T(8,128)} %bitcast.33) | data formatting | bytes 67108864 | tf_op jit(solution)/shard_map/reshape | solution.py:34
  46.2 42.1 %psum.15 = f32[256]{0:T(256)S(1)} all-reduce(f32[256]{0:T(256)S(1)} %get-tuple-element.2), channel_id=1, replica_groups=mesh['mu'=8,'nu'=4] {'mu','nu'}, use_global_device_ids=true, to_apply=%region_1.2 | all-reduce | flops 256 | bytes 2048 | tf_op jit(solution)/shard_map/psum | solution.py:30
  88.3 58.7 %all-reduce.3.cloned.1.call-done = f32[256,512]{1,0:T(8,128)} async-done(((f32[256,512]{1,0:T(8,128)}), f32[256,512]{1,0:T(8,128)}) %all-reduce.3.cloned.1.call-update) | async-done | bytes 524304 | tf_op jit(solution)/shard_map/psum | solution.py:30
  147.1 1.2 multiply_reduce_fusion.1
  148.2 65.5 %multiply_reduce_fusion = (f32[32768]{0:T(1024)S(1)}, f32[32768,256]{0,1:T(8,128)}) fusion(f32[256]{0:T(256)S(1)} %maximum_rsqrt_fusion, f32[32768,256]{0,1:T(8,128)} %copy.20, f32[256,512]{1,0:T(8,128)} %all-reduce.3.cloned.1.call-done, f32[32768,512]{1,0:T(8,128)} %bitcast.1), kind=kOutput, calls=%fused_computation.6 | convolution fusion | flops 51573129216 | bytes 134874112 | tf_op jit(solution)/shard_map/dot_general | solution.py:33
  213.8 30.5 %copy.22 = f32[32,8,128,256]{3,2,1,0:T(8,128)} copy(f32[32,8,128,256]{3,1,2,0:T(8,128)} %bitcast.32) | data formatting | bytes 67108864
  244.3 0.0 copy-done
  244.3 0.0 copy-start.1
  244.3 0.0 copy-start.2
  244.3 23.0 %fusion.6 = f32[256,256,40]{0,2,1:T(8,128)S(1)} fusion(f32[128,256,256]{1,0,2:T(8,128)} %bitcast.31, f32[1024,40]{0,1:T(8,128)S(1)} %copy-done, s32[]{:T(128)S(6)} %select_n.71), kind=kOutput, calls=%fused_computation.13 | convolution fusion | flops 4026531840 | bytes 44060676 | tf_op jit(solution)/shard_map/mp,mnj->jpn/dot_general | solution.py:44
  267.3 10.0 %fusion.2 = f32[256,40,40]{2,1,0:T(8,128)} fusion(f32[256,256,40]{0,2,1:T(8,128)S(1)} %fusion.6, f32[1024,40]{0,1:T(8,128)S(1)} %copy-done, s32[]{:T(128)S(6)} %select_n.72), kind=kOutput, calls=%fused_computation.7 | convolution fusion | flops 1258291200 | bytes 12165124 | tf_op jit(solution)/shard_map/nq,jpn->jpq/dot_general | solution.py:46
  277.3 5.0 %copy.19 = f32[256,40,40]{0,2,1:T(8,128)S(1)} copy(f32[256,40,40]{2,1,0:T(8,128)} %fusion.2) | data formatting | bytes 3276800 | tf_op jit(solution)/shard_map/nq,jpn->jpq/dot_general | solution.py:46
  282.3 0.0 copy-done.1
  282.3 11.0 %gather_fusion.2 = f32[820,256]{1,0:T(8,128)S(1)} fusion(f32[256,40,40]{0,2,1:T(8,128)S(1)} %copy.19, s32[820]{0:T(1024)S(1)} %copy-done.1), kind=kCustom, calls=%fused_computation.2 | custom fusion | bytes 1685920 | tf_op jit(solution)/shard_map/gather | solution.py:47
  293.3 1.2 copy.17
  294.5 0.0 reduce-scatter.5.cloned.1.call-update
  294.6 0.0 reduce-scatter.7.cloned.1.call-start
  294.6 34.6 %reduce-scatter.5.cloned.1.call-done = f32[1,32,820]{2,1,0:T(8,128)} async-done(((f32[8,32,820]{2,1,0:T(8,128)}), f32[1,32,820]{2,1,0:T(8,128)}) %reduce-scatter.5.cloned.1.call-update) | async-done | bytes 104976 | tf_op jit(solution)/shard_map/reduce_scatter | solution.py:51
  329.2 0.0 reduce-scatter.7.cloned.1.call-update
  329.2 0.0 copy-done.2
  329.3 0.7 sub.29
  329.9 21.5 %reduce-scatter.7.cloned.1.call-done = f32[1,8,820]{2,1,0:T(8,128)} async-done(((f32[4,8,820]{2,1,0:T(8,128)}), f32[1,8,820]{2,1,0:T(8,128)}) %reduce-scatter.7.cloned.1.call-update) | async-done | bytes 26256
  (3 shorter events, 0.1 us)
Async XLA Ops:
  7.2 237.1 %copy-start = (f32[1024,40]{0,1:T(8,128)S(1)}, f32[1024,40]{0,1:T(8,128)}, u32[]{:S(2)}) copy-start(f32[1024,40]{0,1:T(8,128)} %param.12) | copy-start | bytes 491524
  7.2 139.9 %all-reduce.3.cloned.1.call-start = ((), (), s32[]{:S(2)}) async-start(), calls=%async_computation.2 | async-start | bytes 1048576 | tf_op jit(solution)/shard_map/psum | solution.py:30
  15.1 314.1 %reduce-scatter.5.cloned.1.call-start = ((), (), s32[]{:S(2)}) async-start(), calls=%async_computation.3 | async-start | bytes 1032192 | tf_op jit(solution)/shard_map/reduce_scatter | solution.py:51
  244.3 38.0 %copy-start.1 = (s32[820]{0:T(1024)S(1)}, s32[820]{0:T(1024)}, u32[]{:S(2)}) copy-start(s32[820]{0:T(1024)} %constant.144) | copy-start | bytes 9844
  244.3 85.0 %copy-start.2 = (f32[128,256]{1,0:T(8,128)S(1)}, f32[128,256]{1,0:T(8,128)}, u32[]{:S(2)}) copy-start(f32[128,256]{1,0:T(8,128)} %param.11) | copy-start | bytes 393220
  294.6 56.9 %reduce-scatter.7.cloned.1.call-start = ((), (), s32[]{:S(2)}) async-start(), calls=%async_computation.4 | async-start | bytes 143360
Sparse Core Ops, SparseCore 0:
  15.2 131.7 all-reduce.2
  294.7 34.4 reduce-scatter.4
  332.0 19.4 reduce-scatter.6
where the time goes:
time: 359 us; the launch traced here: 358 us
  waiting for transfers between devices  115 us (32%)
  matrix products  98.5 us (27%)
  local copies, waits for them, and re-layouts  84.3 us (23%)
  blocking collectives  42.1 us (12%)
  between operations  13.8 us (4%)
  other arithmetic  4.23 us (1%)
    dot_general x1, matrix products, local(): lax.dot_general(flat_vectors, pivot_rows, (((1,), (1,)), ((), ())), preci...  65.5 us
    psum x1, waiting for transfers between devices, local(): pivot_rows, pivot_diag = lax.psum((masked, masked_diag), ('mu', 'nu'))  58.7 us
    psum x1, blocking collectives, local(): pivot_rows, pivot_diag = lax.psum((masked, masked_diag), ('mu', 'nu'))  42.1 us
    reduce_scatter x1, waiting for transfers between devices, local(): summed = lax.psum_scatter(split_mu, 'mu', scatter_dimension=0, tiled=True)  34.6 us
    unnamed x8, local copies, waits for them, and re-layouts  31.5 us
    reshape x1, local copies, waits for them, and re-layouts, local(): pivot_integral_columns.reshape(orbital_rows_mu * cols_nu, pivot_count)  31.1 us
    dot_general x1, matrix products, local(): jnp.einsum('mp,mnj->jpn', basis_left_index, fresh_blocks, precision=precise)  23 us
    unnamed x4, waiting for transfers between devices  21.6 us
  transfers between devices with their start and end apart: 3, of which 3 were waited for; matrix products, arithmetic and copies ran while one was open for 9% of the time, Pallas kernels for 0%

commit v1 on v0

v1 whole, which is shorter than its diff:
```python
import functools

import jax
import jax.numpy as jnp
from jax import lax
from jax.experimental import pallas as pl
from jax.experimental.pallas import tpu as pltpu
from jax.sharding import PartitionSpec as P

f32, bf16 = jnp.float32, jnp.bfloat16


def split(x):
    high = x.astype(bf16)
    return high, (x - high.astype(f32)).astype(bf16)


def mm(a, b):
    return jnp.dot(a, b, preferred_element_type=f32)


def block_kernel(rows, pt_ref, pd_ref, om_ref, on_ref, dg_ref, v_ref, b_ref,
                 full_ref, ud_ref, pcat, scale, oncat, half, tri):
    step = pl.program_id(0)
    _, cols, earlier = v_ref.shape
    active = on_ref.shape[0]
    pivots = b_ref.shape[2]

    @pl.when(step == 0)
    def _():
        pt = pt_ref[...]
        high, low = split(pt)
        pcat[0:earlier] = high
        pcat[earlier:2 * earlier] = high
        pcat[2 * earlier:] = low
        residual = pd_ref[...] - jnp.sum(pt * pt, axis=0, keepdims=True)
        scale[...] = lax.rsqrt(jnp.maximum(residual, 1.0))
        ohigh, olow = split(on_ref[...])
        oncat[0:active] = ohigh
        oncat[active:] = olow

    v = v_ref[...].reshape(rows * cols, earlier)
    vh, vl = split(v)
    update = mm(jnp.concatenate([vh, vl, vh], axis=1), pcat[...])
    fresh = (b_ref[...].reshape(rows * cols, pivots) - update) * scale[...]
    orb = oncat[...]
    for r in range(rows):
        f = fresh[r * cols:(r + 1) * cols]
        fh, fl = split(f)
        both = mm(orb, fh)
        t = both[:active] + both[active:] + mm(orb[:active], fl)
        row = step * rows + r
        for k in range(0, pivots, 128):
            half[k // 128, pl.ds(row * active, active), :] = t[:, k:k + 128]
        sq = f * f
        part = sq[:, :128]
        for k in range(128, pivots, 128):
            part = part + sq[:, k:k + 128]
        total = jnp.sum(part.T, axis=0, keepdims=True)
        ud_ref[pl.ds(row, 1), :] = dg_ref[pl.ds(row, 1), :] - total

    @pl.when(step == pl.num_programs(0) - 1)
    def _():
        count = om_ref.shape[1]
        mh, ml = split(om_ref[...])
        mcat = jnp.concatenate([mh, ml], axis=0)
        for q in range(active):
            tq = jnp.concatenate(
                [half[c, pl.ds(q, count, stride=active), :] for c in range(half.shape[0])], axis=1)
            th, tl = split(tq)
            both = mm(mcat, th)
            g = both[:active] + both[active:] + mm(mh, tl)
            for p in range(q, active):
                tri[p * (p + 1) // 2 + q, :] = g[p]
        pairs = full_ref.shape[1]
        full_ref[...] = tri[...].T[:, :pairs]


def local(earlier_vectors, pivot_integral_columns, diagonal, orbitals, pivots):
    rows_mu, cols_nu, earlier = earlier_vectors.shape
    count = pivots.shape[0]
    ao_count, active = orbitals.shape
    size_mu = lax.axis_size("mu")
    size_nu = lax.axis_size("nu")
    index_mu = lax.axis_index("mu")
    index_nu = lax.axis_index("nu")
    pivot_mu = pivots // ao_count
    pivot_nu = pivots % ao_count
    is_owned = (pivot_mu // rows_mu == index_mu) & (pivot_nu // cols_nu == index_nu)
    local_row = pivot_mu % rows_mu * cols_nu + pivot_nu % cols_nu
    picked = jnp.take(earlier_vectors.reshape(rows_mu * cols_nu, earlier), local_row, axis=0)
    picked_diag = jnp.take(diagonal.reshape(rows_mu * cols_nu), local_row)
    joined = jnp.concatenate(
        [picked, jnp.broadcast_to(picked_diag[:, None], (count, 128))], axis=1)
    joined = lax.psum(jnp.where(is_owned[:, None], joined, 0.0), ("mu", "nu"))
    pivot_t = joined[:, :earlier].T
    pivot_diag = joined[:, earlier][None, :]
    orb_mu = lax.dynamic_slice_in_dim(orbitals, index_mu * rows_mu, rows_mu, 0).T
    orb_nu = lax.dynamic_slice_in_dim(orbitals, index_nu * cols_nu, cols_nu, 0).T

    rows = max(1, min(rows_mu, 1024 // cols_nu))
    pairs = active * (active + 1) // 2
    padded = -(-pairs // 128) * 128
    whole = lambda *shape: pl.BlockSpec(shape, lambda i: (0,) * len(shape))
    full, updated = pl.pallas_call(
        functools.partial(block_kernel, rows),
        grid=(rows_mu // rows,),
        out_shape=(jax.ShapeDtypeStruct((count, pairs), f32),
                   jax.ShapeDtypeStruct((rows_mu, cols_nu), f32)),
        in_specs=[
            whole(earlier, count), whole(1, count), whole(active, rows_mu),
            whole(active, cols_nu), whole(rows_mu, cols_nu),
            pl.BlockSpec((rows, cols_nu, earlier), lambda i: (i, 0, 0)),
            pl.BlockSpec((rows, cols_nu, count), lambda i: (i, 0, 0)),
        ],
        out_specs=(whole(count, pairs), whole(rows_mu, cols_nu)),
        scratch_shapes=[
            pltpu.VMEM((3 * earlier, count), bf16),
            pltpu.VMEM((1, count), f32),
            pltpu.VMEM((2 * active, cols_nu), bf16),
            pltpu.VMEM((count // 128, rows_mu * active, 128), f32),
            pltpu.VMEM((padded, count), f32),
        ],
        compiler_params=pltpu.CompilerParams(
            dimension_semantics=("arbitrary",), vmem_limit_bytes=56 * 1024 * 1024),
    )(pivot_t, pivot_diag, orb_mu, orb_nu, diagonal, earlier_vectors, pivot_integral_columns)

    per_device = count // (size_mu * size_nu)
    split_mu = full.reshape(size_mu, size_nu * per_device, pairs)
    summed = lax.psum_scatter(split_mu, "mu", scatter_dimension=0, tiled=True)
    split_nu = summed.reshape(size_nu, per_device, pairs)
    transformed = lax.psum_scatter(split_nu, "nu", scatter_dimension=0, tiled=True)
    return transformed.reshape(per_device, pairs), updated


def solution(mesh):
    placed = (P("mu", "nu", None), P("mu", "nu", None), P("mu", "nu"), P(), P())
    return jax.shard_map(
        local,
        mesh=mesh,
        in_specs=placed,
        out_specs=(P(("mu", "nu"), None), P("mu", "nu")),
        check_vma=False,
    )
```

time: 359 us -> 272 us (0.76)
  matrix products: 98.5 us -> 0 us
  local copies, waits for them, and re-layouts: 84.3 us -> 10.1 us
  waiting for transfers between devices: 115 us -> 188 us
  Pallas kernels: 0 us -> 56.7 us
  blocking collectives: 42.1 us -> 0 us
    dot_general x3 -> x0, matrix products: 98.5 us -> none  [the longest x1 65.5 us: local(): lax.dot_general(flat_vectors, pivot_rows, (((1,), (1,)), ((), ())), preci...]
    psum x1, waiting for transfers between devices: 58.7 us -> 131 us  [local(): joined = lax.psum(jnp.where(is_owned[:, None], joined, 0.0), ('mu', 'nu'))]
    pallas_call x0 -> x1, Pallas kernels: none -> 56.7 us  [local(): pl.pallas_call(functools.partial(block_kernel, rows), grid=(rows_mu // ro...]
    psum x1 -> x0, blocking collectives: 42.1 us -> none  [local(): pivot_rows, pivot_diag = lax.psum((masked, masked_diag), ('mu', 'nu'))]
    reshape x1 -> x0, local copies, waits for them, and re-layouts: 31.1 us -> none  [local(): pivot_integral_columns.reshape(orbital_rows_mu * cols_nu, pivot_count)]
    unnamed x8 -> x3, local copies, waits for them, and re-layouts: 31.5 us -> 0.98 us
    gather x4 -> x3, local copies, waits for them, and re-layouts: 16.7 us -> 4.68 us  [the longest x2 2.96 us: local(): jnp.take(earlier_vectors.reshape(rows_mu * cols_nu, earlier), local_row,...]
    dot_general x1 -> x0, local copies, waits for them, and re-layouts: 5 us -> none  [local(): jnp.einsum('nq,jpn->jpq', orbit_nu, half_done, precision=precise)]
  transfers between devices with their start and end apart: 3 -> 3, of which waited for: 3 -> 3; matrix products, arithmetic and copies ran while one was open for 9% -> 0% of each run, Pallas kernels for 0% -> 0%
where the time goes in v1:
time: 272 us; the launch traced here: 271 us
  waiting for transfers between devices  188 us (69%)
  Pallas kernels  56.7 us (21%)
  between operations  13.8 us (5%)
  local copies, waits for them, and re-layouts  10.1 us (4%)
    psum x1, waiting for transfers between devices, local(): joined = lax.psum(jnp.where(is_owned[:, None], joined, 0.0), ('mu', 'nu'))  131 us
    pallas_call x1, Pallas kernels, local(): pl.pallas_call(functools.partial(block_kernel, rows), grid=(rows_mu // ro...  56.7 us
    reduce_scatter x1, waiting for transfers between devices, local(): summed = lax.psum_scatter(split_mu, 'mu', scatter_dimension=0, tiled=True)  34.6 us
    unnamed x4, waiting for transfers between devices  22.3 us
  transfers between devices with their start and end apart: 3, of which 3 were waited for; matrix products, arithmetic and copies ran while one was open for 0% of the time, Pallas kernels for 0%

profile of v1, /device:TPU:0, one launch (start us, length us, event | category | flops | bytes accessed | tf_op | source)
XLA Modules:
  0.0 271.3 jit_solution(5566246640200645979)
XLA Ops:
  7.2 0.0 copy-start
  7.2 0.0 all-reduce.3.cloned.1.call-start
  7.2 0.7 compare_and_fusion.1
  8.0 0.7 compare_select_fusion
  8.7 1.0 copy.10
  9.7 1.7 gather_fusion.1
  11.4 2.8 %gather_fusion = f32[256,512]{1,0:T(8,128)S(1)} fusion(f32[32768,512]{1,0:T(8,128)} %bitcast, s32[1024]{0:T(1024)S(1)} %pad_clamp_fusion), kind=kCustom, calls=%fused_computation | custom fusion | bytes 1049600 | tf_op jit(solution)/shard_map/jit(_take)/gather | solution.py:91
  14.2 0.2 copy.9
  14.4 0.9 maximum_select_fusion
  15.3 0.0 all-reduce.3.cloned.1.call-update
  15.3 0.0 reduce-scatter.5.cloned.1.call-start
  15.4 0.0 copy-done
  15.4 0.6 dynamic-slice_bitcast_fusion.1.om_ref
  16.0 0.6 dynamic-slice_bitcast_fusion.on_ref
  16.6 131.3 %all-reduce.3.cloned.1.call-done = f32[256,640]{0,1:T(8,128)} async-done(((f32[256,640]{0,1:T(8,128)}), f32[256,640]{0,1:T(8,128)}) %all-reduce.3.cloned.1.call-update) | async-done | bytes 655376 | tf_op jit(solution)/shard_map/psum | solution.py:95
  147.9 1.3 slice_bitcast_fusion.1.pd_ref
  149.2 1.9 slice_bitcast_fusion.pt_ref
  151.1 56.7 %shard_map.68 = (f32[256,820]{1,0:T(8,128)}, f32[128,256]{1,0:T(8,128)}) custom-call(f32[512,256]{1,0:T(8,128)} %slice_bitcast_fusion.pt_ref, f32[1,256]{1,0:T(1,128)} %slice_bitcast_fusion.1.pd_ref, f32[40,128]{1,0:T(8,128)} %dynamic-slice_bitcast_fusion.1.om_ref, f32[40,256]{1,0:T(8,128)} %dynamic-slice_bitcast_fusion.on_ref, f32[128,256]{1,0:T(8,128)} %dg_ref.1, ...), custom_call_target="tpu_custom_call" | custom-call | tf_op jit(solution)/shard_map/pallas_call | solution.py:105
  207.8 0.0 reduce-scatter.5.cloned.1.call-update
  207.8 0.0 reduce-scatter.7.cloned.1.call-start
  207.9 34.6 %reduce-scatter.5.cloned.1.call-done = f32[1,32,820]{2,1,0:T(8,128)} async-done(((f32[8,32,820]{2,1,0:T(8,128)}), f32[1,32,820]{2,1,0:T(8,128)}) %reduce-scatter.5.cloned.1.call-update) | async-done | bytes 104976 | tf_op jit(solution)/shard_map/reduce_scatter | solution.py:130
  242.5 0.0 reduce-scatter.7.cloned.1.call-update
  242.5 22.3 %reduce-scatter.7.cloned.1.call-done = f32[1,8,820]{2,1,0:T(8,128)} async-done(((f32[4,8,820]{2,1,0:T(8,128)}), f32[1,8,820]{2,1,0:T(8,128)}) %reduce-scatter.7.cloned.1.call-update) | async-done | bytes 26256
  (4 shorter events, 0.1 us)
Async XLA Ops:
  7.2 8.2 %copy-start = (f32[1024,40]{0,1:T(8,128)S(1)}, f32[1024,40]{0,1:T(8,128)}, u32[]{:S(2)}) copy-start(f32[1024,40]{0,1:T(8,128)} %param.8) | copy-start | bytes 491524
  7.2 140.7 %all-reduce.3.cloned.1.call-start = ((), (), s32[]{:S(2)}) async-start(), calls=%async_computation.2 | async-start | bytes 1310720 | tf_op jit(solution)/shard_map/psum | solution.py:95
  15.3 227.1 %reduce-scatter.5.cloned.1.call-start = ((), (), s32[]{:S(2)}) async-start(), calls=%async_computation.3 | async-start | bytes 1032192 | tf_op jit(solution)/shard_map/reduce_scatter | solution.py:130
  207.8 56.9 %reduce-scatter.7.cloned.1.call-start = ((), (), s32[]{:S(2)}) async-start(), calls=%async_computation.4 | async-start | bytes 143360
Sparse Core Ops, SparseCore 0:
  15.5 132.4 all-reduce.2
  208.0 34.4 reduce-scatter.4
  245.3 19.4 reduce-scatter.6
